TPU v7x, 32 devices: a whole 2x2x4 slice. The times are simulated.
32 devices in a mesh: row: 8 (over z, x), col: 4 (over y, core).
Axes of the slice: x: 2, y: 2, z: 4, core: 2. Of those that a mesh axis runs over, the one named last changes fastest.
Arguments:
- factor_u: float32 [1, 8, 2, 4, 512, 128], P(None, 'row', None, 'col'), may hold values from -6 to 6
- factor_v: float32 [1, 8, 2, 4, 512, 128], P(None, 'row', None, 'col'), may hold values from -6 to 6
- near_field: float32 [2, 512, 512], replicated, as said below
- sketch: float32 [2, 512, 128], replicated, may hold values from -6 to 6
- tile_ranks: int32 [3, 1, 8, 2, 4], P(None, None, None, None, 'col'), may hold values from 1 to 128, as said below
Outputs:
- out_u: float32 [1, 8, 2, 4, 512, 128], P(None, 'row', None, 'col')
- out_v: float32 [1, 8, 2, 4, 512, 128], P(None, 'row', None, 'col')
Inputs may be any that keep to these rules, and one draw needn't show every extreme that they name: tile_ranks[0] is at least 16 and equals 128 on every tile (i, i); tile_ranks[1] lies between tile_ranks[0] - tile_ranks[0] // 2 and tile_ranks[0] - max(1, tile_ranks[0] // 4); tile_ranks[2] is at least 1 and at most tile_ranks[1], and when tile_ranks[1] > 1 it is at most tile_ranks[1] - max(1, tile_ranks[1] // 4). The diagonal entries of near_field[0] and near_field[1] lie between 1 and 4.
All inputs are finite; a program needn't handle non-finite values.
Results may differ from a plain program's by a relative error of at most 0.0003.
Values sent between devices are 32-bit elements; how exact they have to be, the bound alone decides.
A program may use at most 64 MiB of HBM per device.

v0:
```python
import math

import jax
import jax.numpy as jnp
from jax import lax
from jax.sharding import PartitionSpec as P

NS_STEPS = 3


highest = lax.Precision.HIGHEST


def from_root(array, axis, root):
    mine = lax.axis_index(axis) == root
    return lax.psum(jnp.where(mine, array, jnp.zeros_like(array)), axis)


def rank_keep(ranks, width):
    return jnp.arange(width, dtype=jnp.int32) < ranks[..., None]


def orthonormal(basis, keeper):
    gram = jnp.einsum("...tk,...tl->...kl", basis, basis, precision=highest)
    unused = 1.0 - keeper.astype(basis.dtype)
    gram = gram + jnp.eye(basis.shape[-1], dtype=basis.dtype) * unused[..., None, :]
    factor = jnp.linalg.cholesky(gram)
    solved = jax.scipy.linalg.solve_triangular(factor, jnp.swapaxes(basis, -1, -2), lower=True)
    return jnp.swapaxes(solved, -1, -2)


def recompress(full_u, full_v, sketch_block, ranks):
    root_order = math.sqrt(full_u.shape[-2])
    keeper = rank_keep(ranks, sketch_block.shape[-1])
    projected = jnp.einsum("...tq,tk->...qk", full_v, sketch_block, precision=highest)
    basis = jnp.einsum("...tq,...qk->...tk", full_u, projected, precision=highest)
    basis = basis * keeper[..., None, :].astype(basis.dtype)
    ortho = orthonormal(orthonormal(basis, keeper), keeper)
    backward = jnp.einsum("...tq,...tk->...qk", full_u, ortho, precision=highest)
    new_v = jnp.einsum("...tq,...qk->...tk", full_v, backward, precision=highest) / root_order
    return (ortho * root_order, new_v)


def update_tiles(cur_u, cur_v, low_u, low_v, up_u, up_v, sketch_block, ranks):
    far_weight = 1.0 / (8.0 * cur_u.shape[-2])
    core_block = far_weight * jnp.einsum("...tk,...tl->...kl", low_v, up_u, precision=highest)
    product_u = jnp.einsum("...tk,...kl->...tl", low_u, core_block, precision=highest)
    full_u = jnp.concatenate([cur_u, -product_u], axis=-1)
    full_v = jnp.concatenate([cur_v, up_v], axis=-1)
    return (product_u, recompress(full_u, full_v, sketch_block, ranks))


def newton_inverse(pivot, start_inverse):
    inverse = jnp.diag(start_inverse)
    twice = 2.0 * jnp.eye(pivot.shape[0], dtype=pivot.dtype)
    for newton_step in range(NS_STEPS):
        inverse = jnp.dot(
            inverse, twice - jnp.dot(pivot, inverse, precision=highest), precision=highest
        )
    return inverse


def body(factor_u, factor_v, near_field, sketch, tile_ranks):
    slot_rows = factor_u.shape[0]
    slot_cols = factor_u.shape[2]
    tile_order = factor_u.shape[4]
    rank_width = factor_u.shape[5]
    row_count = lax.axis_size("row")
    col_count = lax.axis_size("col")
    row_here = lax.axis_index("row")
    col_here = lax.axis_index("col")
    cur_u = factor_u.reshape(slot_rows, slot_cols, tile_order, rank_width)
    cur_v = factor_v.reshape(slot_rows, slot_cols, tile_order, rank_width)
    own_ranks = lax.dynamic_slice_in_dim(tile_ranks, row_here, 1, 2)[:, :, 0, :, 0]
    tile_row = (jnp.arange(slot_rows, dtype=jnp.int32) * row_count + row_here)[:, None]
    tile_col = (jnp.arange(slot_cols, dtype=jnp.int32) * col_count + col_here)[None, :]
    keeper = rank_keep(own_ranks[0], rank_width).astype(jnp.float32)[..., None, :]
    cur_u = cur_u * keeper
    cur_v = cur_v * keeper
    far_weight = 1.0 / (8.0 * tile_order)
    pivot = near_field[0] + far_weight * jnp.dot(cur_u[0, 0], cur_v[0, 0].T, precision=highest)
    for panel in range(2):
        start_inverse = 1.0 / jnp.diagonal(near_field[panel])
        inverse = newton_inverse(pivot, start_inverse)
        inverse = from_root(inverse, "row", panel)
        own_lower = jnp.einsum("st,isk->itk", inverse, cur_v[:, 0], precision=highest)
        low_u, low_v = (from_root(cur_u[:, 0], "col", panel), from_root(own_lower, "col", panel))
        if panel == 0:
            up_u, up_v = (from_root(cur_u[0], "row", 0), from_root(cur_v[0], "row", 0))
        else:
            up_u, up_v = (from_root(cur_u[0], "row", 1), from_root(cur_v[0], "row", 1))
        product_u, fresh_pair = update_tiles(
            cur_u,
            cur_v,
            low_u[:, None],
            low_v[:, None],
            up_u[None],
            up_v[None],
            sketch[panel],
            own_ranks[panel + 1],
        )
        if panel == 0:
            pivot = near_field[1] + far_weight * (
                jnp.dot(cur_u[0, 0], cur_v[0, 0].T, precision=highest)
                - jnp.dot(product_u[0, 0], up_v[0].T, precision=highest)
            )
        chosen = (tile_row > panel) & (tile_col > panel)
        if panel == 0:
            chosen = chosen & jnp.logical_not((tile_row == 1) & (tile_col == 1))
        cur_u = jnp.where(chosen[..., None, None], fresh_pair[0], cur_u)
        cur_v = jnp.where(chosen[..., None, None], fresh_pair[1], cur_v)
        lower_here = (tile_row[:, 0] > panel) & (col_here == panel)
        cur_v = cur_v.at[:, 0].set(jnp.where(lower_here[:, None, None], own_lower, cur_v[:, 0]))
        at_pivot = ((tile_row == panel) & (tile_col == panel))[..., None, None]
        cur_u = jnp.where(at_pivot, 0.0, cur_u)
        cur_v = jnp.where(at_pivot, 0.0, cur_v)
    shape_out = (slot_rows, 1, slot_cols, 1, tile_order, rank_width)
    return (cur_u.reshape(shape_out), cur_v.reshape(shape_out))


def solution(mesh):
    return jax.shard_map(
        body,
        mesh=mesh,
        in_specs=(
            P(None, "row", None, "col", None, None),
            P(None, "row", None, "col", None, None),
            P(),
            P(),
            P(None, None, None, None, "col"),
        ),
        out_specs=(
            P(None, "row", None, "col", None, None),
            P(None, "row", None, "col", None, None),
        ),
        check_vma=False,
    )
```

profile of v0, /device:TPU:0, one launch (start us, length us, event | category | flops | bytes accessed | tf_op | source)
XLA Modules:
  0.0 533.5 jit_solution(3462203937974148620)
XLA Ops:
  7.2 1.2 copy.71
  8.5 1.4 copy.69
  9.9 0.3 fusion.71
  10.3 1.1 bitcast_multiply_fusion.3
  11.4 1.1 fusion.32
  12.5 1.2 slice_bitcast_fusion
  13.7 4.5 gather_fusion
  18.2 2.1 fusion.55
  20.3 1.9 select_subtract_fusion.5
  22.2 1.8 fusion.6
  24.0 1.9 select_subtract_fusion.4
  25.9 1.8 fusion.88
  27.8 1.9 select_subtract_fusion.3
  29.7 2.9 convolution_select_fusion.1
  32.6 0.4 all-reduce.15.cloned.1.call-start
  33.0 8.5 %gather_fusion.1 = f32[512]{0:T(512)S(1)} fusion(f32[512,512]{1,0:T(8,128)} %get-tuple-element.51, s32[512]{0:T(512)S(1)} %bitcast.273), kind=kCustom, calls=%fused_computation.1 | custom fusion | bytes 8192 | tf_op jit(solution)/shard_map/jit(diagonal)/cond/branch_0_fun/gather | solution.py:83
  41.6 1.7 select_bitcast_fusion.3
  43.3 94.7 %all-reduce.11.cloned.1.call-done = (f32[2,512,128]{1,2,0:T(8,128)}, f32[2,512,128]{1,2,0:T(8,128)}, f32[512,512]{1,0:T(8,128)}) async-done(((f32[2,512,128]{1,2,0:T(8,128)}, f32[2,512,128]{1,2,0:T(8,128)}, f32[512,512]{1,0:T(8,128)}), (f32[2,512,128]{1,2,0:T(8,128)}, f32[2,512,128]{1,2,0:T(8,128)}, f32[512,512]{1,0:T(8,128)})) %all-reduce.11.cloned.1.call-update) | async-done | bytes 2097168 | tf_op jit(solution)/shard_map/psum | solution.py:16
  138.0 2.0 convolution_bitcast_fusion.2
  140.0 0.7 select_bitcast_fusion.4
  140.8 3.0 fusion.23
  143.8 29.9 %all-reduce.15.cloned.1.call-done = (f32[512,128]{0,1:T(8,128)}, f32[512,128]{0,1:T(8,128)}) async-done(((f32[512,128]{0,1:T(8,128)}, f32[512,128]{0,1:T(8,128)}), (f32[512,128]{0,1:T(8,128)}, f32[512,128]{0,1:T(8,128)})) %all-reduce.15.cloned.1.call-update) | async-done | bytes 524304 | tf_op jit(solution)/shard_map/psum | solution.py:16
  173.7 1.7 fusion.20
  175.5 1.5 fusion.87
  177.0 2.0 fusion.13
  179.1 1.9 convolution_multiply_fusion.3
  181.0 1.0 convolution_add_fusion.3
  182.1 23.5 %custom-call.16 = f32[1,2,128,128]{3,2,1,0:T(8,128)S(1)} custom-call(f32[1,2,128,128]{3,2,1,0:T(8,128)S(1)} %fusion.63), custom_call_target="Cholesky" | custom-call | tf_op jit(solution)/shard_map/jit(cholesky)/cholesky | solution.py:27
  205.8 19.7 %custom-call.17 = f32[2,1,128,128]{2,3,1,0:T(8,128)S(1)} custom-call(f32[2,1,128,128]{3,2,1,0:T(8,128)S(1)} %select_bitcast_fusion.8), custom_call_target="InvertDiagBlocksLowerTriangular" | custom-call | tf_op jit(solution)/shard_map/jit(_solve_triangular)/vmap()/triangular_solve | solution.py:28
  225.5 0.6 fusion.27
  226.2 0.6 convolution_add_fusion.2
  226.9 23.5 %custom-call.18 = f32[1,2,128,128]{3,2,1,0:T(8,128)S(1)} custom-call(f32[1,2,128,128]{3,2,1,0:T(8,128)S(1)} %fusion.62), custom_call_target="Cholesky" | custom-call | tf_op jit(solution)/shard_map/jit(cholesky)/cholesky | solution.py:27
  250.6 19.8 %custom-call.19 = f32[2,1,128,128]{2,3,1,0:T(8,128)S(1)} custom-call(f32[2,1,128,128]{3,2,1,0:T(8,128)S(1)} %select_bitcast_fusion.7), custom_call_target="InvertDiagBlocksLowerTriangular" | custom-call | tf_op jit(solution)/shard_map/jit(_solve_triangular)/vmap()/triangular_solve | solution.py:28
  270.5 0.6 fusion.67
  271.1 1.2 fusion.24
  272.4 1.8 select_subtract_fusion.2
  274.3 1.9 fusion
  276.1 1.9 select_subtract_fusion.1
  278.0 1.9 fusion.89
  279.8 1.9 select_subtract_fusion
  281.7 3.0 convolution_select_fusion
  284.8 0.7 fusion.16
  285.6 1.3 broadcast_select_fusion
  287.1 0.7 fusion.45
  287.8 101.9 %all-reduce.9.cloned.1.call-done = (f32[1,2,512,128]{2,3,1,0:T(8,128)}, f32[2,512,128]{1,2,0:T(8,128)}, f32[512,512]{1,0:T(8,128)}) async-done(((f32[1,2,512,128]{2,3,1,0:T(8,128)}, f32[2,512,128]{1,2,0:T(8,128)}, f32[512,512]{1,0:T(8,128)}), (f32[1,2,512,128]{2,3,1,0:T(8,128)}, f32[2,512,128]{1,2,0:T(8,128)}, f32[512,512]{1,0:T(8,128)})) %all-reduce.9.cloned.1.call-update) | async-done | bytes 2097168 | tf_op jit(solution)/shard_map/psum | solution.py:16
  389.7 2.0 convolution_bitcast_fusion.1
  391.8 0.7 select_bitcast_fusion.2
  392.6 1.0 fusion.21
  393.6 31.8 %all-reduce.13.cloned.1.call-done = (f32[512,128]{0,1:T(8,128)}, f32[512,128]{0,1:T(8,128)}) async-done(((f32[512,128]{0,1:T(8,128)}, f32[512,128]{0,1:T(8,128)}), (f32[512,128]{0,1:T(8,128)}, f32[512,128]{0,1:T(8,128)})) %all-reduce.13.cloned.1.call-update) | async-done | bytes 524304 | tf_op jit(solution)/shard_map/psum | solution.py:16
  425.4 1.5 fusion.19
  426.9 1.5 fusion.17
  428.5 1.9 convolution_multiply_fusion.1
  430.3 1.0 convolution_add_fusion.1
  431.4 23.7 %custom-call.20 = f32[1,2,128,128]{3,2,1,0:T(8,128)S(1)} custom-call(f32[1,2,128,128]{3,2,1,0:T(8,128)S(1)} %fusion.61), custom_call_target="Cholesky" | custom-call | tf_op jit(solution)/shard_map/jit(cholesky)/cholesky | solution.py:27
  455.4 20.3 %custom-call.21 = f32[2,1,128,128]{2,3,1,0:T(8,128)} custom-call(f32[2,1,128,128]{3,2,1,0:T(8,128)S(1)} %select_bitcast_fusion.6), custom_call_target="InvertDiagBlocksLowerTriangular" | custom-call | tf_op jit(solution)/shard_map/jit(_solve_triangular)/vmap()/triangular_solve | solution.py:28
  475.7 1.5 fusion.25
  477.3 0.6 convolution_add_fusion
  478.0 23.5 %custom-call.22 = f32[1,2,128,128]{3,2,1,0:T(8,128)S(1)} custom-call(f32[1,2,128,128]{3,2,1,0:T(8,128)S(1)} %fusion.60), custom_call_target="Cholesky" | custom-call | tf_op jit(solution)/shard_map/jit(cholesky)/cholesky | solution.py:27
  501.7 20.0 %custom-call.23 = f32[2,1,128,128]{2,3,1,0:T(8,128)S(1)} custom-call(f32[2,1,128,128]{3,2,1,0:T(8,128)S(1)} %select_bitcast_fusion.5), custom_call_target="InvertDiagBlocksLowerTriangular" | custom-call | tf_op jit(solution)/shard_map/jit(_solve_triangular)/vmap()/triangular_solve | solution.py:28
  521.7 0.6 fusion.64
  522.3 1.1 fusion.22
  523.4 0.8 fusion.18
  524.5 1.0 copy.100
  525.5 1.0 copy.99
  (73 shorter events, 2.4 us)
Async XLA Ops:
  7.2 2.8 copy-start.15
  7.2 130.8 %all-reduce.11.cloned.1.call-start = ((), (), s32[]{:S(2)}) async-start(), calls=%async_computation.1 | async-start | bytes 4194304 | tf_op jit(solution)/shard_map/psum | solution.py:16
  8.5 2.9 copy-start.4
  10.3 2.2 copy-start
  32.6 141.1 %all-reduce.15.cloned.1.call-start = ((), (), s32[]{:S(2)}) async-start(), calls=%async_computation.3 | async-start | bytes 1048576 | tf_op jit(solution)/shard_map/psum | solution.py:16
  140.8 249.0 %all-reduce.9.cloned.1.call-start = ((), (), s32[]{:S(2)}) async-start(), calls=%async_computation | async-start | bytes 4194304 | tf_op jit(solution)/shard_map/psum | solution.py:16
  173.7 3.3 copy-start.9
  177.0 4.0 copy-start.7
  177.0 2.1 copy-start.1
  177.0 2.1 copy-start.12
  225.5 45.6 %copy-start.2 = (f32[1,2,512,128]{2,3,1,0:T(8,128)S(1)}, f32[1,2,512,128]{2,3,1,0:T(8,128)}, u32[]{:S(2)}) copy-start(f32[1,2,512,128]{2,3,1,0:T(8,128)} %get-tuple-element.54) | copy-start | bytes 1572868
  225.5 45.6 %copy-start.8 = (f32[1,2,512,128]{2,3,1,0:T(8,128)S(1)}, f32[1,2,512,128]{2,3,1,0:T(8,128)}, u32[]{:S(2)}) copy-start(f32[1,2,512,128]{2,3,1,0:T(8,128)} %copy-done.7) | copy-start | bytes 1572868
  226.8 45.6 %copy-start.3 = (f32[512,512]{1,0:T(8,128)S(1)}, f32[512,512]{1,0:T(8,128)}, u32[]{:S(2)}) copy-start(f32[512,512]{1,0:T(8,128)} %fusion.13) | copy-start | bytes 3145732
  281.7 3.1 copy-start.5
  281.7 3.1 copy-start.6
  281.7 3.1 copy-start.10
  287.0 105.6 %copy-start.14 = (f32[2,512,128]{2,1,0:T(8,128)S(1)}, f32[2,512,128]{2,1,0:T(8,128)}, u32[]{:S(2)}) copy-start(f32[2,512,128]{2,1,0:T(8,128)} %param.15) | copy-start | bytes 1572868
  287.0 138.4 %all-reduce.13.cloned.1.call-start = ((), (), s32[]{:S(2)}) async-start(), calls=%async_computation.2 | async-start | bytes 1048576 | tf_op jit(solution)/shard_map/psum | solution.py:16
  389.7 2.8 copy-start.11
  389.7 35.7 %copy-start.13 = (f32[2,512,128]{1,2,0:T(8,128)S(1)}, f32[2,512,128]{1,2,0:T(8,128)}, u32[]{:S(2)}) copy-start(f32[2,512,128]{1,2,0:T(8,128)} %get-tuple-element.38) | copy-start | bytes 1572868
Sparse Core Ops, SparseCore 0:
  32.7 105.2 all-reduce.10
  141.0 32.6 all-reduce.14
  287.1 102.6 all-reduce.8
  392.6 32.7 all-reduce.12
where the time goes:
time: 543 us; the launch traced here: 534 us
  waiting for transfers between devices  258 us (48%)
  other arithmetic  183 us (34%)
  matrix products  57.1 us (11%)
  local copies, waits for them, and re-layouts  19.6 us (4%)
  between operations  14.9 us (3%)
    psum x4, waiting for transfers between devices, from_root(): return lax.psum(jnp.where(mine, array, jnp.zeros_like(array)), axis)  258 us
    another operation x13, other arithmetic, orthonormal(): factor = jnp.linalg.cholesky(gram)  94.7 us
    another operation x9, other arithmetic, orthonormal(): jax.scipy.linalg.solve_triangular(factor, jnp.swapaxes(basis, -1, -2), lo...  80.2 us
    dot_general x6, matrix products, newton_inverse(): jnp.dot(inverse, twice - jnp.dot(pivot, inverse, precision=highest), prec...  13.3 us
    gather x2, local copies, waits for them, and re-layouts, body(): start_inverse = 1.0 / jnp.diagonal(near_field[panel])  13 us
    dot_general x6, matrix products, newton_inverse(): jnp.dot(pivot, inverse, precision=highest)  11.2 us
  transfers between devices with their start and end apart: 4, of which 4 were waited for; matrix products, arithmetic and copies ran while one was open for 3% of the time, Pallas kernels for 0%

commit v1 on v0

v1 whole, which is shorter than its diff:
```python
import functools
import math

import jax
import jax.numpy as jnp
from jax import lax
from jax.experimental import pallas as pl
from jax.experimental.pallas import tpu as pltpu
from jax.sharding import PartitionSpec as P

NS_STEPS = 3
BLOCK = 16
F32 = jnp.float32
BF16 = jnp.bfloat16
VMEM_SPEC = pl.BlockSpec(memory_space=pltpu.VMEM)
SMEM_SPEC = pl.BlockSpec(memory_space=pltpu.SMEM)
MESH = pl.DeviceIdType.MESH


def split(x):
    high = x.astype(BF16)
    return high, (x - high.astype(F32)).astype(BF16)


def dot_pairs(a, b, contract_b=0):
    dims = (((1,), (contract_b,)), ((), ()))
    ah, al = a
    bh, bl = b
    mm = lambda p, q: lax.dot_general(p, q, dims, preferred_element_type=F32)
    return mm(ah, bh) + (mm(ah, bl) + mm(al, bh))


def dot(a, b):
    return dot_pairs(split(a), split(b))


def dot_nt(a, b):
    return dot_pairs(split(a), split(b), 1)


def dot_tn(a, b):
    return dot_pairs(split(a.T), split(b))


def apply_inverse(matrix, scale, w):
    pair = split(matrix)

    def step(level, x):
        if level == 0:
            return scale * x
        y = step(level - 1, x)
        return step(level - 1, 2.0 * x - dot_pairs(pair, split(y)))

    return step(NS_STEPS, w)


def diagonal_inverse(near):
    n = near.shape[0]
    eye = lax.broadcasted_iota(jnp.int32, (n, n), 0) == lax.broadcasted_iota(jnp.int32, (n, n), 1)
    return 1.0 / jnp.sum(jnp.where(eye, near, 0.0), axis=1, keepdims=True)


def cholesky_inverse(grams, order):
    width = grams[0].shape[1]
    count = len(grams)
    a = [g[:order] for g in grams]
    eye = (
        lax.broadcasted_iota(jnp.int32, (order, width), 0) == lax.broadcasted_iota(jnp.int32, (order, width), 1)
    ).astype(F32)
    w = [eye] * count
    done = [[] for _ in range(count)]
    start = 0
    while start < order:
        size = min(BLOCK, order - start)
        row_id = lax.broadcasted_iota(jnp.int32, (size, width), 0)
        r = [x[:size] for x in a]
        wr = [x[:size] for x in w]
        c = [[jnp.broadcast_to(x[:, start + j : start + j + 1], (size, width)) for j in range(size)] for x in r]
        scale = [jnp.ones((size, width), F32)] * count
        for k in range(size):
            for t in range(count):
                inv = lax.rsqrt(c[t][k][k : k + 1])
                m = jnp.where(row_id > k, c[t][k] * (inv * inv), 0.0)
                for j in range(k + 1, size):
                    c[t][j] = c[t][j] - m * c[t][j][k : k + 1]
                r[t] = r[t] - m * r[t][k : k + 1]
                wr[t] = wr[t] - m * wr[t][k : k + 1]
                scale[t] = jnp.where(row_id == k, inv, scale[t])
        for t in range(count):
            r[t] = r[t] * scale[t]
            wr[t] = wr[t] * scale[t]
            done[t].append(wr[t])
        end = start + size
        if end < order:
            for t in range(count):
                left = r[t].T[end:order]
                upd = jnp.dot(
                    left,
                    jnp.concatenate([r[t], wr[t]], axis=1),
                    precision=lax.Precision.HIGHEST,
                    preferred_element_type=F32,
                )
                a[t] = a[t][size:] - upd[:, :width]
                w[t] = w[t][size:] - upd[:, width:]
        start = end
    tail = width - order
    return [
        jnp.concatenate(d + ([jnp.zeros((tail, width), F32)] if tail else []), axis=0) for d in done
    ]


def orthonormal(bases, ranks, order):
    width = bases[0].shape[1]
    row = lax.broadcasted_iota(jnp.int32, (width, width), 0)
    col = lax.broadcasted_iota(jnp.int32, (width, width), 1)
    grams = []
    for basis, rank in zip(bases, ranks):
        gram = dot_tn(basis, basis)
        grams.append(gram + jnp.where((row == col) & (col >= rank), 1.0, 0.0))
    inverses = cholesky_inverse(grams, order)
    return [dot_nt(basis, inverse) for basis, inverse in zip(bases, inverses)]


def recompress(us, vs, wides, ups, sketch, ranks, order):
    height, width = us[0].shape
    root_order = math.sqrt(height)
    sk = split(sketch)
    bases = []
    for u, v, wide, up, rank in zip(us, vs, wides, ups, ranks):
        here = dot_pairs(split(v.T), sk)
        above = dot_pairs(split(up.T), sk)
        basis = dot(u, here) - dot(wide, above)
        keep = lax.broadcasted_iota(jnp.int32, (height, width), 1) < rank
        bases.append(jnp.where(keep, basis, 0.0))
    orthos = orthonormal(orthonormal(bases, ranks, order), ranks, order)
    out = []
    for u, v, wide, up, ortho in zip(us, vs, wides, ups, orthos):
        o = split(ortho)
        new_v = dot(v, dot_pairs(split(u.T), o)) - dot(up, dot_pairs(split(wide.T), o))
        out.append((ortho * root_order, new_v * (1.0 / root_order)))
    return out


class Tree:
    def __init__(self, root, edges):
        self.root = root
        self.edges = edges


def row_tree(n, source, r, c):
    levels = n // 2
    level, side, e = r // 2, (r + source) % 2, c % 2
    index = lambda l, s: 2 * l + (s + source) % 2
    spine = side == e
    edges = [
        (spine & (level + 1 < levels), (index(level + 1, e), c)),
        (jnp.logical_not(spine) & (level == 1 - e), (index(0, 1), c)),
        (spine & (level >= 1), (index(level, 1 - e), c)),
    ]
    return Tree((level == 0) & (side == 0), edges)


def col_tree(n, source, r, c):
    levels = n // 2
    level, side = c // 2, (c + source) % 2
    index = lambda l, s: 2 * l + (s + source) % 2
    edges = [
        ((side == 0) & (level + 1 < levels), (r, index(level + 1, 0))),
        (side == 0, (r, index(level, 1))),
    ]
    return Tree((level == 0) & (side == 0), edges)


class Piece:
    def __init__(self, tree, own, ref, send, recv, when=None):
        self.tree, self.own, self.ref, self.send, self.recv, self.when = tree, own, ref, send, recv, when

    def both(self, cond):
        return cond if self.when is None else cond & self.when

    def begin(self):
        @pl.when(self.both(self.tree.root))
        def _():
            pltpu.make_async_copy(self.own, self.ref, self.recv).start()

    def copy(self, k, device):
        return pltpu.make_async_remote_copy(
            src_ref=self.ref,
            dst_ref=self.ref,
            send_sem=self.send.at[min(k, 1) if len(self.tree.edges) == 2 else k // 2],
            recv_sem=self.recv,
            device_id=device,
            device_id_type=MESH,
        )

    def forward(self):
        def wait():
            pltpu.make_async_copy(self.ref, self.ref, self.recv).wait()

        if self.when is None:
            wait()
        else:
            pl.when(self.when)(wait)
        for k, (cond, device) in enumerate(self.tree.edges):
            @pl.when(self.both(cond))
            def _(k=k, device=device):
                self.copy(k, device).start()

    def finish(self):
        for k, (cond, device) in enumerate(self.tree.edges):
            @pl.when(self.both(cond))
            def _(k=k, device=device):
                self.copy(k, device).wait_send()


def greet_all(n_row, n_col, r, c):
    barrier = pltpu.get_barrier_semaphore()
    for d in range(1, n_row):
        pl.semaphore_signal(barrier, inc=1, device_id=((r + d) % n_row, c), device_id_type=MESH)
    for d in range(1, n_col):
        pl.semaphore_signal(barrier, inc=1, device_id=(r, (c + d) % n_col), device_id_type=MESH)
    pl.semaphore_wait(barrier, n_row + n_col - 2)


def halves(ref_of):
    return ref_of


def spread_kernel(n_row, n_col, panel, pieces_of, *refs):
    r, c = lax.axis_index("row"), lax.axis_index("col")
    send, recv = refs[-2], refs[-1]
    greet_all(n_row, n_col, r, c)
    pieces_of(n_row, n_col, r, c, refs[:-2], send, recv)


def parts(ref, lead, half):
    view = ref if lead is None else ref.at[lead]
    rows = view.shape[0] // 2
    return view.at[pl.ds(half * rows, rows)]


def first_spread(n_row, n_col, r, c, refs, send, recv):
    u, v, up_u, up_v, low_u, low_v, p_u, p_v, q = refs
    rt = row_tree(n_row, 0, r, c)
    ct = col_tree(n_col, 0, r, c)
    qt = col_tree(n_col, 1, r, c)
    count = [0]

    def piece(tree, own, ref, when=None):
        k = count[0]
        count[0] += 1
        return Piece(tree, own, ref, send.at[k], recv.at[k], when)

    first_row = r == 1
    low = [piece(ct, parts(a, 0, h), parts(b, None, h)) for h in range(2) for a, b in ((u, low_u), (v, low_v))]
    chain = [
        piece(rt, parts(a, t, h), parts(b, t, h))
        for t in range(2)
        for a, b in ((u, up_u), (v, up_v))
        for h in range(2)
    ]
    pivot = [
        piece(ct, parts(a, 0, h), parts(b, None, h)) for a, b in ((up_u, p_u), (up_v, p_v)) for h in range(2)
    ]
    q_own = [piece(qt, parts(a, 0, h), parts(q, k, h), first_row) for k, a in ((0, u), (1, v)) for h in range(2)]
    q_up = [
        piece(qt, parts(a, 0, h), parts(q, k, h), first_row) for k, a in ((2, up_u), (3, up_v)) for h in range(2)
    ]
    for x in chain + low + q_own:
        x.begin()
    for x in low:
        x.forward()
    for k in range(4):
        chain[k].forward()
        pivot[k].begin()
        q_up[k].begin()
    for k in range(4):
        chain[4 + k].forward()
        pivot[k].forward()
    for x in q_own + q_up:
        x.forward()
    for x in low + chain + pivot + q_own + q_up:
        x.finish()


def second_spread(n_row, n_col, r, c, refs, send, recv):
    u, v, y, wide, up_y, up_v, low_u, low_v, up_wide = refs
    rt = row_tree(n_row, 1, r, c)
    ct = col_tree(n_col, 1, r, c)
    count = [0]

    def piece(tree, own, ref, when=None):
        k = count[0]
        count[0] += 1
        return Piece(tree, own, ref, send.at[k], recv.at[k], when)

    low = [piece(ct, parts(a, 0, h), parts(b, None, h)) for h in range(2) for a, b in ((u, low_u), (v, low_v))]
    chain = [
        piece(rt, parts(a, t, h), parts(b, t, h))
        for a, b in ((y, up_y), (v, up_v))
        for t in range(2)
        for h in range(2)
    ]
    extra = [piece(rt, parts(wide, None, h), parts(up_wide, None, h), c == 1) for h in range(2)]
    for x in chain + low + extra:
        x.begin()
    for x in low[:2] + chain[:2] + low[2:] + chain[2:] + extra:
        x.forward()
    for x in low + chain + extra:
        x.finish()


def spread(mesh_shape, body, pieces, collective_id, inputs, out_shapes):
    n_row, n_col = mesh_shape
    return pl.pallas_call(
        functools.partial(spread_kernel, n_row, n_col, 0, body),
        out_shape=[jax.ShapeDtypeStruct(s, F32) for s in out_shapes],
        in_specs=[VMEM_SPEC] * len(inputs),
        out_specs=[VMEM_SPEC] * len(out_shapes),
        scratch_shapes=[pltpu.SemaphoreType.DMA((pieces, 2)), pltpu.SemaphoreType.DMA((pieces,))],
        compiler_params=pltpu.CompilerParams(collective_id=collective_id, has_side_effects=True),
    )(*inputs)


def first_panel(n_row, n_col, order, ranks, u, v, up_u, up_v, low_u, low_v, p_u, p_v, q, near, sketch, ou, ov, oy, ow):
    r, c = lax.axis_index("row"), lax.axis_index("col")
    far = 1.0 / (8.0 * u.shape[1])
    pivot_t = near[0].T + far * dot_nt(p_v[...], p_u[...])
    lower = apply_inverse(pivot_t, diagonal_inverse(near[0]), low_v[...])
    lower_t = split(lower.T)
    lead = split(low_u[...])
    wide_of = lambda up: dot_pairs(lead, split(far * dot_pairs(lower_t, split(up))))
    us, vs = [u[t] for t in range(2)], [v[t] for t in range(2)]
    ups = [up_v[t] for t in range(2)]
    wides = [wide_of(up_u[t]) for t in range(2)]
    fresh = recompress(us, vs, wides, ups, sketch[0], [ranks[1, t] for t in range(2)], order)
    for t in range(2):
        j = t * n_col + c
        chosen = (r > 0) & (j > 0) & jnp.logical_not((r == 1) & (j == 1))
        pivot_here = (r == 0) & (j == 0)
        lower_here = (r > 0) & (j == 0)
        ou[t] = jnp.where(pivot_here, 0.0, jnp.where(chosen, fresh[t][0], us[t]))
        ov[t] = jnp.where(pivot_here, 0.0, jnp.where(lower_here, lower, jnp.where(chosen, fresh[t][1], vs[t])))

    @pl.when(r == 1)
    def _():
        wide = wide_of(q[2])
        pivot = near[1] + far * (dot_nt(q[0], q[1]) - dot_nt(wide, q[3]))
        scale = diagonal_inverse(near[1])
        width = u.shape[2]
        y = apply_inverse(pivot, scale, jnp.concatenate([ou[0], ou[1]], axis=1))
        oy[0] = jnp.where(c == 1, q[0], y[:, :width])
        oy[1] = y[:, width:]
        ow[...] = wide


def second_panel(n_row, n_col, order, ranks, u, v, up_y, up_v, low_u, low_v, up_wide, old_v, near, sketch, ou, ov):
    r, c = lax.axis_index("row"), lax.axis_index("col")
    far = 1.0 / (8.0 * u.shape[1])
    lower_t = split(low_v[...].T)
    lead = split(low_u[...])
    us, vs = [u[t] for t in range(2)], [v[t] for t in range(2)]
    ups = [up_v[t] for t in range(2)]
    wides = [dot_pairs(lead, split(far * dot_pairs(lower_t, split(up_y[t])))) for t in range(2)]
    fresh = recompress(us, vs, wides, ups, sketch[1], [ranks[2, t] for t in range(2)], order)
    for t in range(2):
        j = t * n_col + c
        chosen = (r > 1) & (j > 1)
        pivot_here = (r == 1) & (j == 1)
        ou[t] = jnp.where(pivot_here, 0.0, jnp.where(chosen, fresh[t][0], us[t]))
        ov[t] = jnp.where(pivot_here, 0.0, jnp.where(chosen, fresh[t][1], vs[t]))

    @pl.when((c == 1) & (r > 1))
    def _():
        pivot_t = near[1].T + far * (dot_nt(up_v[0], up_y[0]) - dot_nt(old_v[0], up_wide[...]))
        ov[0] = apply_inverse(pivot_t, diagonal_inverse(near[1]), v[0])


def panel_call(body, out_shapes, inputs):
    return pl.pallas_call(
        body,
        out_shape=[jax.ShapeDtypeStruct(s, F32) for s in out_shapes],
        in_specs=[SMEM_SPEC] + [VMEM_SPEC] * (len(inputs) - 1),
        out_specs=[VMEM_SPEC] * len(out_shapes),
        compiler_params=pltpu.CompilerParams(vmem_limit_bytes=60 * 1024 * 1024),
    )(*inputs)


def body(n_row, n_col, factor_u, factor_v, near_field, sketch, tile_ranks):
    tiles, height, width = factor_u.shape[2], factor_u.shape[4], factor_u.shape[5]
    row_here = lax.axis_index("row")
    ranks = lax.dynamic_slice_in_dim(tile_ranks, row_here, 1, 2).reshape(3, tiles)
    keep = (jnp.arange(width, dtype=jnp.int32) < ranks[0][:, None]).astype(F32)[:, None, :]
    u = factor_u.reshape(tiles, height, width) * keep
    v = factor_v.reshape(tiles, height, width) * keep
    pair, one = (tiles, height, width), (height, width)
    shape = (n_row, n_col)
    order_1 = width - max(1, width // 4)
    order_2 = order_1 - max(1, order_1 // 4)
    up_u, up_v, low_u, low_v, p_u, p_v, q = spread(
        shape, first_spread, 24, 0, (u, v), (pair, pair, one, one, one, one, (4, height, width))
    )
    u1, v1, y, wide = panel_call(
        functools.partial(first_panel, n_row, n_col, order_1),
        (pair, pair, pair, one),
        (ranks, u, v, up_u, up_v, low_u, low_v, p_u, p_v, q, near_field, sketch),
    )
    up_y, up_v1, low_u1, low_v1, up_wide = spread(
        shape, second_spread, 14, 1, (u1, v1, y, wide), (pair, pair, one, one, one)
    )
    u2, v2 = panel_call(
        functools.partial(second_panel, n_row, n_col, order_2),
        (pair, pair),
        (ranks, u1, v1, up_y, up_v1, low_u1, low_v1, up_wide, up_v, near_field, sketch),
    )
    shape_out = (1, 1, tiles, 1, height, width)
    return (u2.reshape(shape_out), v2.reshape(shape_out))


def solution(mesh):
    return jax.shard_map(
        functools.partial(body, mesh.shape["row"], mesh.shape["col"]),
        mesh=mesh,
        in_specs=(
            P(None, "row", None, "col", None, None),
            P(None, "row", None, "col", None, None),
            P(),
            P(),
            P(None, None, None, None, "col"),
        ),
        out_specs=(
            P(None, "row", None, "col", None, None),
            P(None, "row", None, "col", None, None),
        ),
        check_vma=False,
    )
```

time: 543 us -> 137 us (0.25)
  the two profiles are of different devices: /device:TPU:0 before, /device:TPU:28 now
where the time goes in v1:
time: 137 us; the launch traced here: 136 us
  Pallas kernels  131 us (96%)
  other arithmetic  2.31 us (2%)
  local copies, waits for them, and re-layouts  1.74 us (1%)
    pallas_call x2, Pallas kernels, spread(): pl.pallas_call(functools.partial(spread_kernel, n_row, n_col, 0, body), o...  95.2 us
    pallas_call x2, Pallas kernels, panel_call(): pl.pallas_call(body, out_shape=[jax.ShapeDtypeStruct(s, F32) for s in out...  36 us

profile of v1, /device:TPU:28, one launch (start us, length us, event | category | flops | bytes accessed | tf_op | source)
XLA Modules:
  0.0 135.9 jit_solution(2960841513209567412)
XLA Ops:
  0.6 0.0 copy-start
  0.6 0.7 copy-done
  1.3 0.2 dynamic-slice_reduce_fusion
  1.5 0.1 compare_convert_fusion
  1.6 0.1 constant_dynamic-slice_fusion
  1.7 0.1 copy.12
  1.8 0.7 copy.14.ranks
  2.5 2.2 %bitcast_multiply_fusion = (f32[2,512,128]{2,1,0:T(8,128)}, f32[2,512,128]{2,1,0:T(8,128)}) fusion(f32[1,1,2,1,512,128]{5,4,3,2,1,0:T(8,128)} %param.6, f32[2,128]{1,0:T(2,128)S(1)} %compare_convert_fusion, f32[1,1,2,1,512,128]{5,4,3,2,1,0:T(8,128)} %param.5), kind=kLoop, calls=%fused_computation | loop fusion | flops 262144 | bytes 2098176 | tf_op jit(solution)/shard_map/mul | solution.py:395
  4.7 40.2 %shard_map.68 = (f32[2,512,128]{2,1,0:T(8,128)}, f32[2,512,128]{2,1,0:T(8,128)}, f32[512,128]{1,0:T(8,128)}, f32[512,128]{1,0:T(8,128)}, f32[512,128]{1,0:T(8,12...) custom-call(f32[2,512,128]{2,1,0:T(8,128)} %get-tuple-element.43.refs_0_.u, f32[2,512,128]{2,1,0:T(8,128)} %get-tuple-element.42.refs_1_.v), custom_call_target="tpu_custom_call" | custom-call | tf_op jit(solution)/shard_map/pallas_call | solution.py:315
  44.9 22.7 %shard_map.69 = (f32[2,512,128]{2,1,0:T(8,128)}, f32[2,512,128]{2,1,0:T(8,128)}, f32[2,512,128]{2,1,0:T(8,128)}, f32[512,128]{1,0:T(8,128)}) custom-call(s32[3,2]{1,0:T(4,128)} %copy.14.ranks, f32[2,512,128]{2,1,0:T(8,128)} %get-tuple-element.43.refs_0_.u, f32[2,512,128]{2,1,0:T(8,128)} %get-tuple-element.42.refs_1_.v, ...), custom_call_target="tpu_custom_call" | custom-call | tf_op jit(solution)/shard_map/pallas_call | solution.py:380
  67.6 55.0 %shard_map.70 = (f32[2,512,128]{2,1,0:T(8,128)}, f32[2,512,128]{2,1,0:T(8,128)}, f32[512,128]{1,0:T(8,128)}, f32[512,128]{1,0:T(8,128)}, f32[512,128]{1,0:T(8,128)}) custom-call(f32[2,512,128]{2,1,0:T(8,128)} %get-tuple-element.27.refs_0_.u, f32[2,512,128]{2,1,0:T(8,128)} %get-tuple-element.28.refs_1_.v, f32[2,512,128]{2,1,0:T(8,128)} %get-tuple-element.29.refs_2_, ...), custom_call_target="tpu_custom_call" | custom-call | tf_op jit(solution)/shard_map/pallas_call | solution.py:315
  122.7 13.2 %shard_map.71 = (f32[2,512,128]{2,1,0:T(8,128)}, f32[2,512,128]{2,1,0:T(8,128)}) custom-call(s32[3,2]{1,0:T(4,128)} %copy.14.ranks, f32[2,512,128]{2,1,0:T(8,128)} %get-tuple-element.27.refs_0_.u, f32[2,512,128]{2,1,0:T(8,128)} %get-tuple-element.28.refs_1_.v, f32[2,512,128]{2,1,0:T(8,128)} %get-tuple-element.31.up_y, ...), custom_call_target="tpu_custom_call" | custom-call | tf_op jit(solution)/shard_map/pallas_call | solution.py:380
Async XLA Ops:
  0.6 0.7 copy-start

commit v2 on v1

v2 whole, which is shorter than its diff:
```python
import functools
import math

import jax
import jax.numpy as jnp
from jax import lax
from jax.experimental import pallas as pl
from jax.experimental.pallas import tpu as pltpu
from jax.sharding import PartitionSpec as P

NS_STEPS = 3
BLOCK = 16
F32 = jnp.float32
BF16 = jnp.bfloat16
VMEM_SPEC = pl.BlockSpec(memory_space=pltpu.VMEM)
SMEM_SPEC = pl.BlockSpec(memory_space=pltpu.SMEM)
MESH = pl.DeviceIdType.MESH


def split(x):
    high = x.astype(BF16)
    return high, (x - high.astype(F32)).astype(BF16)


def dot_pairs(a, b, contract_b=0):
    dims = (((1,), (contract_b,)), ((), ()))
    ah, al = a
    bh, bl = b
    mm = lambda p, q: lax.dot_general(p, q, dims, preferred_element_type=F32)
    return mm(ah, bh) + (mm(ah, bl) + mm(al, bh))


def dot(a, b):
    return dot_pairs(split(a), split(b))


def dot_nt(a, b):
    return dot_pairs(split(a), split(b), 1)


def dot_tn(a, b):
    return dot_pairs(split(a.T), split(b))


def apply_inverse(matrix, scale, w):
    pair = split(matrix)

    def step(level, x):
        if level == 0:
            return scale * x
        y = step(level - 1, x)
        return step(level - 1, 2.0 * x - dot_pairs(pair, split(y)))

    return step(NS_STEPS, w)


def diagonal_inverse(near):
    n = near.shape[0]
    eye = lax.broadcasted_iota(jnp.int32, (n, n), 0) == lax.broadcasted_iota(jnp.int32, (n, n), 1)
    return 1.0 / jnp.sum(jnp.where(eye, near, 0.0), axis=1, keepdims=True)


def cholesky_inverse(grams, order):
    width = grams[0].shape[1]
    count = len(grams)
    eye = (
        lax.broadcasted_iota(jnp.int32, (order, width), 0) == lax.broadcasted_iota(jnp.int32, (order, width), 1)
    ).astype(F32)
    rest = [jnp.concatenate([g[:order], eye], axis=1) for g in grams]
    done = []
    start = 0
    while start < order:
        size = min(BLOCK, order - start)
        row_id = lax.broadcasted_iota(jnp.int32, (1, size, width), 1)
        rows = jnp.stack([x[:size] for x in rest])
        cols = jnp.stack(
            [
                jnp.stack([jnp.broadcast_to(x[:size, start + j : start + j + 1], (size, width)) for x in rest])
                for j in range(size)
            ]
        )
        scale = jnp.ones((count, size, width), F32)
        for k in range(size):
            lead = cols[0]
            inv = lax.rsqrt(lead[:, k : k + 1])
            m = jnp.where(row_id > k, lead * (inv * inv), 0.0)
            if k + 1 < size:
                cols = cols[1:]
                cols = cols - m[None] * cols[:, :, k : k + 1]
            rows = rows - jnp.concatenate([m, m], axis=2) * rows[:, k : k + 1]
            scale = jnp.where(row_id == k, inv, scale)
        rows = rows * jnp.concatenate([scale, scale], axis=2)
        done.append(rows[:, :, width:])
        end = start + size
        if end < order:
            rest = [
                rest[t][size:]
                - jnp.dot(
                    rows[t][:, :width].T[end:order],
                    rows[t],
                    precision=lax.Precision.HIGHEST,
                    preferred_element_type=F32,
                )
                for t in range(count)
            ]
        start = end
    if order < width:
        done.append(jnp.zeros((count, width - order, width), F32))
    inverses = jnp.concatenate(done, axis=1)
    return [inverses[t] for t in range(count)]


def orthonormal(bases, ranks, order):
    width = bases[0].shape[1]
    row = lax.broadcasted_iota(jnp.int32, (width, width), 0)
    col = lax.broadcasted_iota(jnp.int32, (width, width), 1)
    grams = []
    for basis, rank in zip(bases, ranks):
        gram = dot_tn(basis, basis)
        grams.append(gram + jnp.where((row == col) & (col >= rank), 1.0, 0.0))
    inverses = cholesky_inverse(grams, order)
    return [dot_nt(basis, inverse) for basis, inverse in zip(bases, inverses)]


def recompress(us, vs, wides, ups, sketch, ranks, order):
    height, width = us[0].shape
    root_order = math.sqrt(height)
    sk = split(sketch)
    bases = []
    for u, v, wide, up, rank in zip(us, vs, wides, ups, ranks):
        here = dot_pairs(split(v.T), sk)
        above = dot_pairs(split(up.T), sk)
        basis = dot(u, here) - dot(wide, above)
        keep = lax.broadcasted_iota(jnp.int32, (height, width), 1) < rank
        bases.append(jnp.where(keep, basis, 0.0))
    orthos = orthonormal(orthonormal(bases, ranks, order), ranks, order)
    out = []
    for u, v, wide, up, ortho in zip(us, vs, wides, ups, orthos):
        o = split(ortho)
        new_v = dot(v, dot_pairs(split(u.T), o)) - dot(up, dot_pairs(split(wide.T), o))
        out.append((ortho * root_order, new_v * (1.0 / root_order)))
    return out


class Tree:
    def __init__(self, root, edges):
        self.root = root
        self.edges = edges


def row_tree(n, source, r, c):
    levels = n // 2
    level, side, e = r // 2, (r + source) % 2, c % 2
    index = lambda l, s: 2 * l + (s + source) % 2
    spine = side == e
    edges = [
        (spine & (level + 1 < levels), (index(level + 1, e), c)),
        (jnp.logical_not(spine) & (level == 1 - e), (index(0, 1), c)),
        (spine & (level >= 1), (index(level, 1 - e), c)),
    ]
    return Tree((level == 0) & (side == 0), edges)


def col_tree(n, source, r, c):
    levels = n // 2
    level, side = c // 2, (c + source) % 2
    index = lambda l, s: 2 * l + (s + source) % 2
    edges = [
        ((side == 0) & (level + 1 < levels), (r, index(level + 1, 0))),
        (side == 0, (r, index(level, 1))),
    ]
    return Tree((level == 0) & (side == 0), edges)


class Piece:
    def __init__(self, tree, own, ref, send, recv, when=None):
        self.tree, self.own, self.ref, self.send, self.recv, self.when = tree, own, ref, send, recv, when

    def both(self, cond):
        return cond if self.when is None else cond & self.when

    def begin(self):
        @pl.when(self.both(self.tree.root))
        def _():
            pltpu.make_async_copy(self.own, self.ref, self.recv).start()

    def copy(self, k, device):
        return pltpu.make_async_remote_copy(
            src_ref=self.ref,
            dst_ref=self.ref,
            send_sem=self.send.at[min(k, 1) if len(self.tree.edges) == 2 else k // 2],
            recv_sem=self.recv,
            device_id=device,
            device_id_type=MESH,
        )

    def forward(self, only=None):
        both = lambda cond: self.both(cond if only is None else cond & only)

        def wait():
            pltpu.make_async_copy(self.ref, self.ref, self.recv).wait()

        if self.when is None and only is None:
            wait()
        else:
            pl.when(self.when if only is None else self.both(only))(wait)
        for k, (cond, device) in enumerate(self.tree.edges):
            @pl.when(both(cond))
            def _(k=k, device=device):
                self.copy(k, device).start()

    def finish(self):
        for k, (cond, device) in enumerate(self.tree.edges):
            @pl.when(self.both(cond))
            def _(k=k, device=device):
                self.copy(k, device).wait_send()


def greet_all(n_row, n_col, r, c):
    barrier = pltpu.get_barrier_semaphore()
    for d in range(1, n_row):
        pl.semaphore_signal(barrier, inc=1, device_id=((r + d) % n_row, c), device_id_type=MESH)
    for d in range(1, n_col):
        pl.semaphore_signal(barrier, inc=1, device_id=(r, (c + d) % n_col), device_id_type=MESH)
    pl.semaphore_wait(barrier, n_row + n_col - 2)


def parts(ref, lead, half):
    view = ref if lead is None else ref.at[lead]
    rows = view.shape[0] // 2
    return view.at[pl.ds(half * rows, rows)]


def kernel(n_row, n_col, order_1, order_2, ranks, u, v, near, sketch, out_u, out_v, *scratch):
    (up_u, up_v, low_u, low_v, p_u, p_v, q, u1, v1, y, wide_own, up_y, up_v1, low_u1, low_v1, up_wide, send, recv) = scratch
    r, c = lax.axis_index("row"), lax.axis_index("col")
    far = 1.0 / (8.0 * u.shape[1])
    width = u.shape[2]
    greet_all(n_row, n_col, r, c)
    rt0, rt1 = row_tree(n_row, 0, r, c), row_tree(n_row, 1, r, c)
    ct0, ct1 = col_tree(n_col, 0, r, c), col_tree(n_col, 1, r, c)
    pieces = []

    def piece(tree, own, ref, when=None):
        k = len(pieces)
        pieces.append(Piece(tree, own, ref, send.at[k], recv.at[k], when))
        return pieces[-1]

    two = range(2)
    first_row = r == 1
    low = [piece(ct0, parts(a, 0, h), parts(b, None, h)) for h in two for a, b in ((u, low_u), (v, low_v))]
    chain = [piece(rt0, parts(a, t, h), parts(b, t, h)) for t in two for a, b in ((u, up_u), (v, up_v)) for h in two]
    pivot = [piece(ct0, parts(a, 0, h), parts(b, None, h)) for a, b in ((up_u, p_u), (up_v, p_v)) for h in two]
    q_own = [piece(ct1, parts(a, 0, h), parts(q, k, h), first_row) for k, a in ((0, u), (1, v)) for h in two]
    q_up = [piece(ct1, parts(a, 0, h), parts(q, k, h), first_row) for k, a in ((2, up_u), (3, up_v)) for h in two]
    low1 = [piece(ct1, parts(a, 0, h), parts(b, None, h)) for h in two for a, b in ((u1, low_u1), (v1, low_v1))]
    chain_v = [piece(rt1, parts(v1, t, h), parts(up_v1, t, h)) for t in two for h in two]
    chain_y = [piece(rt1, parts(y, t, h), parts(up_y, t, h)) for t in two for h in two]
    extra = [piece(rt1, parts(wide_own, None, h), parts(up_wide, None, h), c == 1) for h in two]

    for x in chain + low + q_own:
        x.begin()
    for x in low:
        x.forward()
    for k in range(4):
        chain[k].forward()
        pivot[k].begin()
        q_up[k].begin()
    for k in range(4):
        chain[4 + k].forward()
        pivot[k].forward()
    for x in q_own + q_up:
        x.forward(c == 1)
    pivot_t = near[0].T + far * dot_nt(p_v[...], p_u[...])
    lower = apply_inverse(pivot_t, diagonal_inverse(near[0]), low_v[...])
    for x in q_own + q_up:
        x.forward(c != 1)
    lower_t = split(lower.T)
    lead = split(low_u[...])
    wide_of = lambda up: dot_pairs(lead, split(far * dot_pairs(lower_t, split(up))))
    us, vs = [u[t] for t in two], [v[t] for t in two]
    fresh = recompress(
        us, vs, [wide_of(up_u[t]) for t in two], [up_v[t] for t in two], sketch[0], [ranks[1, t] for t in two], order_1
    )
    for t in two:
        j = t * n_col + c
        chosen = (r > 0) & (j > 0) & jnp.logical_not((r == 1) & (j == 1))
        pivot_here = (r == 0) & (j == 0)
        lower_here = (r > 0) & (j == 0)
        u1[t] = jnp.where(pivot_here, 0.0, jnp.where(chosen, fresh[t][0], us[t]))
        v1[t] = jnp.where(pivot_here, 0.0, jnp.where(lower_here, lower, jnp.where(chosen, fresh[t][1], vs[t])))

    @pl.when(first_row)
    def _():
        wide_own[...] = wide_of(q[2])

    for x in low1 + chain_v + extra:
        x.begin()
    for x in low1 + chain_v + extra:
        x.forward()

    @pl.when(first_row)
    def _():
        pivot_1 = near[1] + far * (dot_nt(q[0], q[1]) - dot_nt(wide_own[...], q[3]))
        applied = apply_inverse(pivot_1, diagonal_inverse(near[1]), jnp.concatenate([u1[0], u1[1]], axis=1))
        y[0] = jnp.where(c == 1, q[0], applied[:, :width])
        y[1] = applied[:, width:]

    for x in chain_y:
        x.begin()
    for x in chain_y:
        x.forward()
    lower_t1 = split(low_v1[...].T)
    lead_1 = split(low_u1[...])
    us, vs = [u1[t] for t in two], [v1[t] for t in two]
    wides = [dot_pairs(lead_1, split(far * dot_pairs(lower_t1, split(up_y[t])))) for t in two]
    fresh = recompress(us, vs, wides, [up_v1[t] for t in two], sketch[1], [ranks[2, t] for t in two], order_2)
    for t in two:
        j = t * n_col + c
        chosen = (r > 1) & (j > 1)
        pivot_here = (r == 1) & (j == 1)
        out_u[t] = jnp.where(pivot_here, 0.0, jnp.where(chosen, fresh[t][0], us[t]))
        out_v[t] = jnp.where(pivot_here, 0.0, jnp.where(chosen, fresh[t][1], vs[t]))

    @pl.when((c == 1) & (r > 1))
    def _():
        pivot_1t = near[1].T + far * (dot_nt(up_v1[0], up_y[0]) - dot_nt(up_v[0], up_wide[...]))
        out_v[0] = apply_inverse(pivot_1t, diagonal_inverse(near[1]), v1[0])

    for x in pieces:
        x.finish()


def body(n_row, n_col, factor_u, factor_v, near_field, sketch, tile_ranks):
    tiles, height, width = factor_u.shape[2], factor_u.shape[4], factor_u.shape[5]
    row_here = lax.axis_index("row")
    ranks = lax.dynamic_slice_in_dim(tile_ranks, row_here, 1, 2).reshape(3, tiles)
    keep = (jnp.arange(width, dtype=jnp.int32) < ranks[0][:, None]).astype(F32)[:, None, :]
    u = factor_u.reshape(tiles, height, width) * keep
    v = factor_v.reshape(tiles, height, width) * keep
    pair, one = (tiles, height, width), (height, width)
    order_1 = width - max(1, width // 4)
    order_2 = order_1 - max(1, order_1 // 4)
    buffers = [pair, pair, one, one, one, one, (4, height, width), pair, pair, pair, one, pair, pair, one, one, one]
    pieces = 38
    out_u, out_v = pl.pallas_call(
        functools.partial(kernel, n_row, n_col, order_1, order_2),
        out_shape=[jax.ShapeDtypeStruct(pair, F32)] * 2,
        in_specs=[SMEM_SPEC] + [VMEM_SPEC] * 4,
        out_specs=[VMEM_SPEC] * 2,
        scratch_shapes=[pltpu.VMEM(s, F32) for s in buffers]
        + [pltpu.SemaphoreType.DMA((pieces, 2)), pltpu.SemaphoreType.DMA((pieces,))],
        compiler_params=pltpu.CompilerParams(
            collective_id=0, has_side_effects=True, vmem_limit_bytes=60 * 1024 * 1024
        ),
    )(ranks, u, v, near_field, sketch)
    shape_out = (1, 1, tiles, 1, height, width)
    return (out_u.reshape(shape_out), out_v.reshape(shape_out))


def solution(mesh):
    return jax.shard_map(
        functools.partial(body, mesh.shape["row"], mesh.shape["col"]),
        mesh=mesh,
        in_specs=(
            P(None, "row", None, "col", None, None),
            P(None, "row", None, "col", None, None),
            P(),
            P(),
            P(None, None, None, None, "col"),
        ),
        out_specs=(
            P(None, "row", None, "col", None, None),
            P(None, "row", None, "col", None, None),
        ),
        check_vma=False,
    )
```

time: 137 us -> 107 us (0.78)
  Pallas kernels: 131 us -> 97.8 us
  local copies, waits for them, and re-layouts: 1.74 us -> 5.47 us
    pallas_call x4 -> x1, Pallas kernels: 131 us -> 97.8 us  [body(): pl.pallas_call(functools.partial(kernel, n_row, n_col, order_1, order_2),...]
    unnamed x2 -> x4, local copies, waits for them, and re-layouts: 0.68 us -> 4.42 us
where the time goes in v2:
time: 107 us; the launch traced here: 106 us
  Pallas kernels  97.8 us (91%)
  local copies, waits for them, and re-layouts  5.47 us (5%)
  other arithmetic  2.31 us (2%)
    pallas_call x1, Pallas kernels, body(): pl.pallas_call(functools.partial(kernel, n_row, n_col, order_1, order_2),...  97.8 us
    unnamed x4, local copies, waits for them, and re-layouts  4.42 us
    mul x1, other arithmetic, body(): v = factor_v.reshape(tiles, height, width) * keep  2.24 us

profile of v2, /device:TPU:28, one launch (start us, length us, event | category | flops | bytes accessed | tf_op | source)
XLA Modules:
  0.0 106.2 jit_solution(6637536542018024053)
XLA Ops:
  0.6 0.0 copy-start
  0.6 0.7 copy-done
  1.3 0.2 dynamic-slice_reduce_fusion
  1.5 0.1 compare_convert_fusion
  1.6 0.1 constant_dynamic-slice_fusion
  1.7 0.1 copy.11
  1.8 0.7 copy.12.ranks
  2.5 2.2 %bitcast_multiply_fusion = (f32[2,512,128]{2,1,0:T(8,128)}, f32[2,512,128]{2,1,0:T(8,128)}) fusion(f32[1,1,2,1,512,128]{5,4,3,2,1,0:T(8,128)} %param.6, f32[2,128]{1,0:T(2,128)S(1)} %compare_convert_fusion, f32[1,1,2,1,512,128]{5,4,3,2,1,0:T(8,128)} %param.5), kind=kLoop, calls=%fused_computation | loop fusion | flops 262144 | bytes 2098176 | tf_op jit(solution)/shard_map/mul | solution.py:340
  4.7 97.8 %shard_map.68 = (f32[2,512,128]{2,1,0:T(8,128)}, f32[2,512,128]{2,1,0:T(8,128)}) custom-call(s32[3,2]{1,0:T(4,128)} %copy.12.ranks, f32[2,512,128]{2,1,0:T(8,128)} %get-tuple-element.11.u, f32[2,512,128]{2,1,0:T(8,128)} %get-tuple-element.10.v, f32[2,512,512]{2,1,0:T(8,128)} %near.1, f32[2,512,128]{2,1,0:T(8,128)} %sketch.1), custom_call_target="tpu_custom_call" | custom-call | tf_op jit(solution)/shard_map/pallas_call | solution.py:346
  102.5 1.9 %copy.17 = f32[1,1,2,1,512,128]{5,4,3,2,1,0:T(8,128)} copy(f32[1,1,2,1,512,128]{5,4,3,2,1,0:T(8,128)} %bitcast.12) | data formatting | bytes 1048576
  104.4 1.9 %copy.18 = f32[1,1,2,1,512,128]{5,4,3,2,1,0:T(8,128)} copy(f32[1,1,2,1,512,128]{5,4,3,2,1,0:T(8,128)} %bitcast.11) | data formatting | bytes 1048576
Async XLA Ops:
  0.6 0.7 copy-start

commit v3 on v2

--- a/solution.py
+++ b/solution.py
@@ -148,14 +148,14 @@
         self.edges = edges
 
 
-def row_tree(n, source, r, c):
+def row_tree(n, source, r, c, direct=False):
     levels = n // 2
     level, side, e = r // 2, (r + source) % 2, c % 2
     index = lambda l, s: 2 * l + (s + source) % 2
     spine = side == e
     edges = [
         (spine & (level + 1 < levels), (index(level + 1, e), c)),
-        (jnp.logical_not(spine) & (level == 1 - e), (index(0, 1), c)),
+        ((level == 0) & (side == 0) if direct else jnp.logical_not(spine) & (level == 1 - e), (index(0, 1), c)),
         (spine & (level >= 1), (index(level, 1 - e), c)),
     ]
     return Tree((level == 0) & (side == 0), edges)
@@ -188,7 +188,7 @@
         return pltpu.make_async_remote_copy(
             src_ref=self.ref,
             dst_ref=self.ref,
-            send_sem=self.send.at[min(k, 1) if len(self.tree.edges) == 2 else k // 2],
+            send_sem=self.send.at[min(k, 1)],
             recv_sem=self.recv,
             device_id=device,
             device_id_type=MESH,
@@ -225,19 +225,20 @@
     pl.semaphore_wait(barrier, n_row + n_col - 2)
 
 
-def parts(ref, lead, half):
+def parts(ref, lead, part, count=2):
     view = ref if lead is None else ref.at[lead]
-    rows = view.shape[0] // 2
-    return view.at[pl.ds(half * rows, rows)]
+    rows = view.shape[0] // count
+    return view.at[pl.ds(part * rows, rows)]
 
 
 def kernel(n_row, n_col, order_1, order_2, ranks, u, v, near, sketch, out_u, out_v, *scratch):
-    (up_u, up_v, low_u, low_v, p_u, p_v, q, u1, v1, y, wide_own, up_y, up_v1, low_u1, low_v1, up_wide, send, recv) = scratch
+    (up_u, up_v, low_u, low_v, p_u, p_v, q, u1, v1, y, wide_own, up_y, up_v1, low_u1, low_v1, up_pivot, lower_1, send, recv) = scratch
     r, c = lax.axis_index("row"), lax.axis_index("col")
     far = 1.0 / (8.0 * u.shape[1])
     width = u.shape[2]
     greet_all(n_row, n_col, r, c)
     rt0, rt1 = row_tree(n_row, 0, r, c), row_tree(n_row, 1, r, c)
+    rt0_first = row_tree(n_row, 0, r, c, True)
     ct0, ct1 = col_tree(n_col, 0, r, c), col_tree(n_col, 1, r, c)
     pieces = []
 
@@ -249,14 +250,30 @@
     two = range(2)
     first_row = r == 1
     low = [piece(ct0, parts(a, 0, h), parts(b, None, h)) for h in two for a, b in ((u, low_u), (v, low_v))]
-    chain = [piece(rt0, parts(a, t, h), parts(b, t, h)) for t in two for a, b in ((u, up_u), (v, up_v)) for h in two]
+    chain = [
+        piece(tree, parts(a, t, h), parts(b, t, h))
+        for t, tree in ((0, rt0_first), (1, rt0))
+        for a, b in ((u, up_u), (v, up_v))
+        for h in two
+    ]
     pivot = [piece(ct0, parts(a, 0, h), parts(b, None, h)) for a, b in ((up_u, p_u), (up_v, p_v)) for h in two]
     q_own = [piece(ct1, parts(a, 0, h), parts(q, k, h), first_row) for k, a in ((0, u), (1, v)) for h in two]
     q_up = [piece(ct1, parts(a, 0, h), parts(q, k, h), first_row) for k, a in ((2, up_u), (3, up_v)) for h in two]
     low1 = [piece(ct1, parts(a, 0, h), parts(b, None, h)) for h in two for a, b in ((u1, low_u1), (v1, low_v1))]
-    chain_v = [piece(rt1, parts(v1, t, h), parts(up_v1, t, h)) for t in two for h in two]
-    chain_y = [piece(rt1, parts(y, t, h), parts(up_y, t, h)) for t in two for h in two]
-    extra = [piece(rt1, parts(wide_own, None, h), parts(up_wide, None, h), c == 1) for h in two]
+    chain_v = [
+        piece(rt1, parts(v1, t, h), parts(up_v1, t, h), when) for t, when in ((0, c != 1), (1, None)) for h in two
+    ]
+    quarters = range(4)
+    chain_y = [
+        piece(rt1, parts(y, t, h, 4), parts(up_y, t, h, 4), when)
+        for t, when in ((0, c != 1), (1, None))
+        for h in quarters
+    ]
+    extra = [
+        piece(rt1, parts(a, lead, h), parts(up_pivot, k, h), c == 1)
+        for k, a, lead in ((0, wide_own, None), (1, u1, 0), (2, v1, 0))
+        for h in two
+    ]
 
     for x in chain + low + q_own:
         x.begin()
@@ -294,16 +311,26 @@
     def _():
         wide_own[...] = wide_of(q[2])
 
-    for x in low1 + chain_v + extra:
+    for x in low1 + extra + chain_v:
         x.begin()
-    for x in low1 + chain_v + extra:
+    for x in low1 + extra:
         x.forward()
+    for x in chain_v:
+        x.forward(first_row)
+
+    @pl.when((c == 1) & (r > 1))
+    def _():
+        pivot_1t = near[1].T + far * (dot_nt(up_pivot[2], up_pivot[1]) - dot_nt(up_v[0], up_pivot[0]))
+        lower_1[...] = apply_inverse(pivot_1t, diagonal_inverse(near[1]), v1[0])
+
+    for x in chain_v:
+        x.forward(r != 1)
 
     @pl.when(first_row)
     def _():
         pivot_1 = near[1] + far * (dot_nt(q[0], q[1]) - dot_nt(wide_own[...], q[3]))
         applied = apply_inverse(pivot_1, diagonal_inverse(near[1]), jnp.concatenate([u1[0], u1[1]], axis=1))
-        y[0] = jnp.where(c == 1, q[0], applied[:, :width])
+        y[0] = applied[:, :width]
         y[1] = applied[:, width:]
 
     for x in chain_y:
@@ -318,14 +345,12 @@
     for t in two:
         j = t * n_col + c
         chosen = (r > 1) & (j > 1)
-        pivot_here = (r == 1) & (j == 1)
-        out_u[t] = jnp.where(pivot_here, 0.0, jnp.where(chosen, fresh[t][0], us[t]))
-        out_v[t] = jnp.where(pivot_here, 0.0, jnp.where(chosen, fresh[t][1], vs[t]))
+        out_u[t] = jnp.where(chosen, fresh[t][0], us[t])
+        out_v[t] = jnp.where(chosen, fresh[t][1], vs[t])
 
     @pl.when((c == 1) & (r > 1))
     def _():
-        pivot_1t = near[1].T + far * (dot_nt(up_v1[0], up_y[0]) - dot_nt(up_v[0], up_wide[...]))
-        out_v[0] = apply_inverse(pivot_1t, diagonal_inverse(near[1]), v1[0])
+        out_v[0] = lower_1[...]
 
     for x in pieces:
         x.finish()
@@ -341,8 +366,8 @@
     pair, one = (tiles, height, width), (height, width)
     order_1 = width - max(1, width // 4)
     order_2 = order_1 - max(1, order_1 // 4)
-    buffers = [pair, pair, one, one, one, one, (4, height, width), pair, pair, pair, one, pair, pair, one, one, one]
-    pieces = 38
+    buffers = [pair, pair, one, one, one, one, (4, height, width), pair, pair, pair, one, pair, pair, one, one, (3, height, width), one]
+    pieces = 46
     out_u, out_v = pl.pallas_call(
         functools.partial(kernel, n_row, n_col, order_1, order_2),
         out_shape=[jax.ShapeDtypeStruct(pair, F32)] * 2,
@@ -354,6 +379,9 @@
             collective_id=0, has_side_effects=True, vmem_limit_bytes=60 * 1024 * 1024
         ),
     )(ranks, u, v, near_field, sketch)
+    tile_col = jnp.arange(tiles, dtype=jnp.int32) * n_col + lax.axis_index("col")
+    stays = jnp.logical_not((row_here == 1) & (tile_col == 1))[:, None, None]
+    out_u, out_v = jnp.where(stays, out_u, 0.0), jnp.where(stays, out_v, 0.0)
     shape_out = (1, 1, tiles, 1, height, width)
     return (out_u.reshape(shape_out), out_v.reshape(shape_out))
 

time: 107 us -> 103 us (0.963)
  local copies, waits for them, and re-layouts: 5.47 us -> 1.69 us
  other arithmetic: 2.31 us -> 4.62 us
  Pallas kernels: 97.8 us -> 96.2 us
    unnamed x4 -> x2, local copies, waits for them, and re-layouts: 4.42 us -> 0.66 us
    unnamed x0 -> x1, other arithmetic: none -> 2.3 us
    pallas_call x1, Pallas kernels: 97.8 us -> 96.2 us  [body(): pl.pallas_call(functools.partial(kernel, n_row, n_col, order_1, order_2),...]
where the time goes in v3:
time: 103 us
  Pallas kernels  96.2 us (93%)
  other arithmetic  4.62 us (4%)
  local copies, waits for them, and re-layouts  1.69 us (2%)
    pallas_call x1, Pallas kernels, body(): pl.pallas_call(functools.partial(kernel, n_row, n_col, order_1, order_2),...  96.2 us
    unnamed x1, other arithmetic  2.3 us
    mul x1, other arithmetic, body(): v = factor_v.reshape(tiles, height, width) * keep  2.24 us

profile of v3, /device:TPU:28, one launch (start us, length us, event | category | flops | bytes accessed | tf_op | source)
XLA Modules:
  0.0 103.2 jit_solution(11666346599844697299)
XLA Ops:
  0.6 0.0 copy-start
  0.7 0.7 copy-done
  1.3 0.2 dynamic-slice_reduce_fusion
  1.5 0.1 compare_convert_fusion
  1.6 0.1 constant_dynamic-slice_fusion
  1.7 0.1 copy.11
  1.8 0.7 copy.12.ranks
  2.4 2.2 %bitcast_multiply_fusion = (f32[2,512,128]{2,1,0:T(8,128)}, f32[2,512,128]{2,1,0:T(8,128)}) fusion(f32[1,1,2,1,512,128]{5,4,3,2,1,0:T(8,128)} %param.6, f32[2,128]{1,0:T(2,128)S(1)} %compare_convert_fusion, f32[1,1,2,1,512,128]{5,4,3,2,1,0:T(8,128)} %param.5), kind=kLoop, calls=%fused_computation | loop fusion | flops 262144 | bytes 2098176 | tf_op jit(solution)/shard_map/mul | solution.py:365
  4.7 96.2 %shard_map.68 = (f32[2,512,128]{2,1,0:T(8,128)}, f32[2,512,128]{2,1,0:T(8,128)}) custom-call(s32[3,2]{1,0:T(4,128)} %copy.12.ranks, f32[2,512,128]{2,1,0:T(8,128)} %get-tuple-element.11.u, f32[2,512,128]{2,1,0:T(8,128)} %get-tuple-element.10.v, f32[2,512,512]{2,1,0:T(8,128)} %near.1, f32[2,512,128]{2,1,0:T(8,128)} %sketch.1), custom_call_target="tpu_custom_call" | custom-call | tf_op jit(solution)/shard_map/pallas_call | solution.py:371
  100.9 2.3 %select_bitcast_fusion = (f32[1,1,2,1,512,128]{5,4,3,2,1,0:T(8,128)}, f32[1,1,2,1,512,128]{5,4,3,2,1,0:T(8,128)}) fusion(f32[2,512,128]{2,1,0:T(8,128)} %get-tuple-element.5, pred[2]{0:T(512)(128)(4,1)S(1)} %and_not_fusion, f32[2,512,128]{2,1,0:T(8,128)} %get-tuple-element.4), kind=kLoop, calls=%fused_computation.2 | loop fusion | flops 262144 | bytes 2097154
  (1 shorter events, 0.0 us)
Async XLA Ops:
  0.6 0.7 copy-start

commit v4 on v3

--- a/solution.py
+++ b/solution.py
@@ -290,8 +290,6 @@
         x.forward(c == 1)
     pivot_t = near[0].T + far * dot_nt(p_v[...], p_u[...])
     lower = apply_inverse(pivot_t, diagonal_inverse(near[0]), low_v[...])
-    for x in q_own + q_up:
-        x.forward(c != 1)
     lower_t = split(lower.T)
     lead = split(low_u[...])
     wide_of = lambda up: dot_pairs(lead, split(far * dot_pairs(lower_t, split(up))))
@@ -306,6 +304,9 @@
         lower_here = (r > 0) & (j == 0)
         u1[t] = jnp.where(pivot_here, 0.0, jnp.where(chosen, fresh[t][0], us[t]))
         v1[t] = jnp.where(pivot_here, 0.0, jnp.where(lower_here, lower, jnp.where(chosen, fresh[t][1], vs[t])))
+
+    for x in q_own + q_up:
+        x.forward(c != 1)
 
     @pl.when(first_row)
     def _():

time: 103 us -> 103 us (level)
  no operation moved by 1% of the time
where the time goes in v4:
time: 103 us
  Pallas kernels  96.2 us (93%)
  other arithmetic  4.62 us (4%)
  local copies, waits for them, and re-layouts  1.69 us (2%)
    pallas_call x1, Pallas kernels, body(): pl.pallas_call(functools.partial(kernel, n_row, n_col, order_1, order_2),...  96.2 us
    unnamed x1, other arithmetic  2.3 us
    mul x1, other arithmetic, body(): v = factor_v.reshape(tiles, height, width) * keep  2.24 us

profile of v4, /device:TPU:28, one launch (start us, length us, event | category | flops | bytes accessed | tf_op | source)
XLA Modules:
  0.0 103.2 jit_solution(12824698702524580316)
XLA Ops:
  0.6 0.0 copy-start
  0.7 0.7 copy-done
  1.3 0.2 dynamic-slice_reduce_fusion
  1.5 0.1 compare_convert_fusion
  1.6 0.1 constant_dynamic-slice_fusion
  1.7 0.1 copy.11
  1.8 0.7 copy.12.ranks
  2.4 2.2 %bitcast_multiply_fusion = (f32[2,512,128]{2,1,0:T(8,128)}, f32[2,512,128]{2,1,0:T(8,128)}) fusion(f32[1,1,2,1,512,128]{5,4,3,2,1,0:T(8,128)} %param.6, f32[2,128]{1,0:T(2,128)S(1)} %compare_convert_fusion, f32[1,1,2,1,512,128]{5,4,3,2,1,0:T(8,128)} %param.5), kind=kLoop, calls=%fused_computation | loop fusion | flops 262144 | bytes 2098176 | tf_op jit(solution)/shard_map/mul | solution.py:366
  4.7 96.2 %shard_map.68 = (f32[2,512,128]{2,1,0:T(8,128)}, f32[2,512,128]{2,1,0:T(8,128)}) custom-call(s32[3,2]{1,0:T(4,128)} %copy.12.ranks, f32[2,512,128]{2,1,0:T(8,128)} %get-tuple-element.11.u, f32[2,512,128]{2,1,0:T(8,128)} %get-tuple-element.10.v, f32[2,512,512]{2,1,0:T(8,128)} %near.1, f32[2,512,128]{2,1,0:T(8,128)} %sketch.1), custom_call_target="tpu_custom_call" | custom-call | tf_op jit(solution)/shard_map/pallas_call | solution.py:372
  100.9 2.3 %select_bitcast_fusion = (f32[1,1,2,1,512,128]{5,4,3,2,1,0:T(8,128)}, f32[1,1,2,1,512,128]{5,4,3,2,1,0:T(8,128)}) fusion(f32[2,512,128]{2,1,0:T(8,128)} %get-tuple-element.5, pred[2]{0:T(512)(128)(4,1)S(1)} %and_not_fusion, f32[2,512,128]{2,1,0:T(8,128)} %get-tuple-element.4), kind=kLoop, calls=%fused_computation.2 | loop fusion | flops 262144 | bytes 2097154
  (1 shorter events, 0.0 us)
Async XLA Ops:
  0.6 0.7 copy-start
